TPU v7x, 32 devices: a whole 2x2x4 slice. The times are simulated.
32 devices in a mesh: ta: 16 (over z, y, x), sa: 2 (over core).
Axes of the slice: x: 2, y: 2, z: 4, core: 2. Of those that a mesh axis runs over, the one named last changes fastest.
Arguments:
- rhs: float32 [1, 2, 40, 16, 2, 128], P(None, None, None, 'ta', 'sa'), may hold values from -6 to 6
- links: bfloat16 [4, 2, 40, 40, 16, 2, 128], P(None, None, None, None, 'ta', 'sa'), may hold values from -0.625 to 0.625
- clover: bfloat16 [2, 40, 40, 16, 2, 128], P(None, None, None, 'ta', 'sa'), may hold values from -1 to 7
- mr_steps: int32 [16, 2, 2], P('ta', 'sa'), may hold values from 2 to 3
Outputs:
- solution: float32 [1, 2, 40, 16, 2, 128], P(None, None, None, 'ta', 'sa')
- residual: float32 [1, 2, 40, 16, 2, 128], P(None, None, None, 'ta', 'sa')
All inputs are finite; a program needn't handle non-finite values.
Results may differ from a plain program's by a relative error of at most 0.0003.
Values sent between devices are 32-bit elements; how exact they have to be, the bound alone decides.
A program may use at most 128 MiB of HBM per device.

v0:
```python
import functools

import jax
import jax.numpy as jnp
from jax import lax
from jax.experimental import pallas as pl
from jax.experimental.pallas import tpu as pltpu
from jax.sharding import PartitionSpec as P

LZ = 4
LY = 4
LX = 4
MR_MAX = 3
SWEEPS = 2
PHASES = 2 * SWEEPS
UNROLL = 4
MESH = pl.DeviceIdType.MESH


def kernel(
    nt,
    nz,
    rhs_ref,
    links_ref,
    clover_ref,
    steps_ref,
    x_ref,
    r_ref,
    lk,
    cl,
    g,
    rs,
    xs,
    s_ref,
    e_ref,
    acc,
    gv,
    f_ref,
    sbuf,
    rbuf,
    csem,
    ssem,
    rsem,
):
    dof, lanes = rhs_ref.shape[1:]
    half = lanes // 2
    tiles = dof // 8
    ta = lax.axis_index("ta")
    sa = lax.axis_index("sa")
    t_next, t_prev = lax.rem(ta + 1, nt), lax.rem(ta + nt - 1, nt)
    z_next, z_prev = lax.rem(sa + 1, nz), lax.rem(sa + nz - 1, nz)

    copies = [
        pltpu.make_async_copy(links_ref.at[d], lk.at[d], csem.at[d]) for d in range(4)
    ] + [pltpu.make_async_copy(clover_ref, cl, csem.at[4])]
    for d in (2, 1, 3, 4, 0):
        copies[d].start()

    barrier = pltpu.get_barrier_semaphore()
    for where_to in ({"ta": t_next}, {"ta": t_prev}, {"sa": z_next}, {"sa": z_prev}):
        pl.semaphore_signal(barrier, inc=1, device_id=where_to, device_id_type=MESH)

    shape = (dof, lanes)
    lane = lax.broadcasted_iota(jnp.int32, shape, 1)
    row = lax.broadcasted_iota(jnp.int32, shape, 0)
    signs = jnp.where(row < dof // 2, 1.0, -1.0).astype(jnp.float32)
    low = lane < half
    site = lane % half
    zpos = site // (LY * LX)
    ypos = site // LX % LY
    xpos = site % LX
    z_last, z_first = zpos == LZ - 1, zpos == 0
    y_last, y_first = ypos == LY - 1, ypos == 0
    x_last, x_first = xpos == LX - 1, xpos == 0
    zero = jnp.zeros(shape, jnp.float32)
    plane = LY * LX

    def roll(v, by):
        return pltpu.roll(v, by % lanes, 1)

    for c in range(2):
        v = rhs_ref[c]
        w = roll(v, half)
        rs[0, c] = jnp.where(low, v, w)
        rs[1, c] = jnp.where(low, w, v)
        xs[0, c] = zero
        xs[1, c] = zero

    def prepare(plain, rolled, groups):
        def body(i, carry):
            for c in range(2):
                b = roll(rolled(c, i).astype(jnp.float32), half)
                for source, group in zip(plain, groups):
                    a = source(c, i).astype(jnp.float32)
                    g[group, 0, c, i] = jnp.where(low, a, b)
                    g[group, 1, c, i] = jnp.where(low, b, a)
            return carry

        lax.fori_loop(0, dof, body, 0)

    def link(d):
        return lambda c, i: lk[d, c, i]

    copies[2].wait()
    copies[1].wait()
    prepare([link(2)], link(1), [0])
    copies[3].wait()
    copies[4].wait()
    copies[0].wait()
    prepare([lambda c, i: cl[c, i], link(0)], link(3), [1, 2])
    prepare([link(0)], link(1), [3])

    def fold(v):
        total = v[0:8]
        for t in range(1, tiles):
            total = total + v[8 * t : 8 * t + 8]
        return total

    def gathered(slots):
        parts = []
        for t in range(tiles):
            total = None
            for slot in slots:
                for k in range(8):
                    piece = f_ref[slot, pl.ds(8 * 8 * t + k, 8, stride=8), :]
                    total = piece if total is None else total + piece
            parts.append(total)
        return jnp.concatenate(parts, axis=0)

    def sweep_matrices(forward, forward_half, inputs, backward, backward_half, slot):
        vr, vi = inputs
        vs = vr + vi
        shared = backward == forward

        def one(i, carry):
            mr, mi = g[forward, forward_half, 0, i], g[forward, forward_half, 1, i]
            ms = mr + mi
            p1 = fold(mr * vr)
            p2 = fold(mi * vi)
            p3 = fold(ms * vs)
            at = pl.multiple_of(8 * i, 8)
            f_ref[slot, pl.ds(at, 8), :] = p1 - p2
            f_ref[slot + 1, pl.ds(at, 8), :] = p3 - p1 - p2
            if backward is None:
                return carry
            if not shared:
                mr, mi = g[backward, backward_half, 0, i], g[backward, backward_half, 1, i]
                ms = mr + mi
            b1, b2, b3 = carry
            br = gv[0, pl.ds(i, 1), :]
            bi = gv[1, pl.ds(i, 1), :]
            bd = gv[2, pl.ds(i, 1), :]
            return (b1 + mr * br, b2 + mi * bi, b3 + ms * bd)

        def body(outer, carry):
            for inner in range(UNROLL):
                carry = one(outer * UNROLL + inner, carry)
            return carry

        start = 0 if backward is None else (zero, zero, zero)
        got = lax.fori_loop(0, dof // UNROLL, body, start)
        if backward is None:
            return None
        b1, b2, b3 = got
        return -signs * (b1 + b2), -signs * (b1 - b2 - b3)

    def phase(ph, token):
        h = lax.rem(ph + sa, 2)
        other = 1 - h
        limit = steps_ref[h]
        first = (lane // half) == h
        h_is_0 = (lane * 0 + h) == 0

        for c in range(2):
            s_ref[c] = rs[h, c]
            e_ref[c] = zero
            acc[0, c] = zero
            acc[1, c] = zero

        def step(k, carry):
            sr, si = s_ref[0], s_ref[1]
            gr, gi = signs * sr, signs * si
            gv[0] = gr
            gv[1] = gi
            gv[2] = gr - gi

            def ahead0(v):
                n = -v
                ya = jnp.where(y_last, roll(n, (LY - 1) * LX), roll(n, -LX))
                za = jnp.where(z_last, 0.0, roll(n, -plane))
                return jnp.where(first, ya, za)

            def ahead1(v):
                n = -v
                xa = jnp.where(x_last, roll(n, LX - 1), roll(n, -1))
                return jnp.where(first, v, xa)

            back0 = sweep_matrices(0, h, (ahead0(sr), ahead0(si)), 0, h, 0)
            back2 = sweep_matrices(1, h, (ahead1(sr), ahead1(si)), 2, h, 2)
            q = []
            for c in range(2):
                b, d = back0[c], back2[c]
                yb = jnp.where(y_first, roll(b, -(LY - 1) * LX), roll(b, LX))
                zb = jnp.where(z_first, 0.0, roll(b, plane))
                xb = jnp.where(x_first, roll(d, -(LX - 1)), roll(d, 1))
                u = gathered((c, 2 + c)) + jnp.where(first, yb, zb) + jnp.where(first, 0.0, xb)
                q.append(u + roll(u, half))
            qr, qi = q

            def total(v):
                return jnp.sum(jnp.sum(fold(v), axis=0, keepdims=True), axis=1, keepdims=True)

            numer_real = total(qr * sr + qi * si)
            numer_imag = total(qr * si - qi * sr)
            denom = total(qr * qr + qi * qi) + 2e-6
            live = (lane * 0 + limit) > k
            ar = jnp.where(live, jnp.broadcast_to(numer_real / denom, shape), 0.0)
            ai = jnp.where(live, jnp.broadcast_to(numer_imag / denom, shape), 0.0)
            e_ref[0] += ar * sr - ai * si
            e_ref[1] += ar * si + ai * sr
            s_ref[0] = sr - (ar * qr - ai * qi)
            s_ref[1] = si - (ar * qi + ai * qr)
            for n, (vr, vi) in enumerate((back0, back2)):
                acc[n, 0] += ar * vr - ai * vi
                acc[n, 1] += ar * vi + ai * vr
            return carry

        lax.fori_loop(0, MR_MAX, step, 0)

        er, ei = e_ref[0], e_ref[1]
        bz = [-jnp.where(first, roll(acc[0, c], half), acc[0, c]) for c in range(2)]
        bt = [-jnp.where(first, acc[1, c], roll(acc[1, c], half)) for c in range(2)]
        packed = jnp.where(low, er, ei)
        sbuf[ph, 0] = jnp.where(h_is_0, packed, jnp.where(low, bt[0], bt[1]))
        sbuf[ph, 1] = packed
        sbuf[ph, 2] = jnp.where(low, bz[0], bz[1])

        @pl.when(ph == 0)
        def _():
            pl.semaphore_wait(barrier, 4)

        target = lax.rem(ta + nt + 2 * h - 1, nt)
        sends = []
        for n, where_to in enumerate(({"ta": target}, {"sa": z_prev}, {"sa": z_next})):
            send = pltpu.make_async_remote_copy(
                src_ref=sbuf.at[ph, n],
                dst_ref=rbuf.at[ph, n],
                send_sem=ssem.at[ph, n],
                recv_sem=rsem.at[ph, n],
                device_id=where_to,
                device_id_type=MESH,
            )
            send.start()
            sends.append(send)

        for c, ec in enumerate((er, ei)):
            xs[h, c] += ec
            rs[h, c] = s_ref[c]

        for send in sends:
            send.wait()

        def unpack(n):
            m = rbuf[ph, n]
            w = roll(m, half)
            return jnp.where(low, m, w), jnp.where(low, w, m)

        got_t, got_e, got_b = unpack(0), unpack(1), unpack(2)
        inputs = []
        for c, ec in enumerate((er, ei)):
            tin = jnp.where(h_is_0, got_t[c], ec)
            zin = jnp.where(z_last, roll(got_e[c], -plane), 0.0)
            inputs.append(jnp.where(first, zin, tin))
        sweep_matrices(3, other, inputs, None, None, 0)
        for c in range(2):
            u = gathered((c,))
            behind = jnp.where(h_is_0, bt[c], got_t[c])
            zb = jnp.where(z_first, roll(got_b[c], plane), 0.0)
            rs[other, c] += u + roll(u, half) + behind + zb
        return token

    lax.fori_loop(0, PHASES, phase, 0)

    for c in range(2):
        x_ref[c] = jnp.where(low, xs[0, c], xs[1, c])
        r_ref[c] = jnp.where(low, rs[0, c], rs[1, c])


def shards(nt, nz, rhs, links, clover, mr_steps):
    dof, lanes = rhs.shape[2], rhs.shape[-1]
    f32 = jnp.float32
    vmem = pl.BlockSpec(memory_space=pltpu.VMEM)
    hbm = pl.BlockSpec(memory_space=pl.ANY)
    x, r = pl.pallas_call(
        functools.partial(kernel, nt, nz),
        out_shape=[jax.ShapeDtypeStruct((2, dof, lanes), f32)] * 2,
        in_specs=[vmem, hbm, hbm, pl.BlockSpec(memory_space=pltpu.SMEM)],
        out_specs=[vmem, vmem],
        scratch_shapes=[
            pltpu.VMEM((4, 2, dof, dof, lanes), jnp.bfloat16),
            pltpu.VMEM((2, dof, dof, lanes), jnp.bfloat16),
            pltpu.VMEM((4, 2, 2, dof, dof, lanes), f32),
            pltpu.VMEM((2, 2, dof, lanes), f32),
            pltpu.VMEM((2, 2, dof, lanes), f32),
            pltpu.VMEM((2, dof, lanes), f32),
            pltpu.VMEM((2, dof, lanes), f32),
            pltpu.VMEM((2, 2, dof, lanes), f32),
            pltpu.VMEM((3, dof, lanes), f32),
            pltpu.VMEM((4, 8 * dof, lanes), f32),
            pltpu.VMEM((PHASES, 3, dof, lanes), f32),
            pltpu.VMEM((PHASES, 3, dof, lanes), f32),
            pltpu.SemaphoreType.DMA((5,)),
            pltpu.SemaphoreType.DMA((PHASES, 3)),
            pltpu.SemaphoreType.DMA((PHASES, 3)),
        ],
        compiler_params=pltpu.CompilerParams(
            collective_id=0, has_side_effects=True, vmem_limit_bytes=48 * 1024 * 1024
        ),
    )(
        rhs.reshape(2, dof, lanes),
        links.reshape(4, 2, dof, dof, lanes),
        clover.reshape(2, dof, dof, lanes),
        mr_steps.reshape(2),
    )
    return x.reshape(rhs.shape), r.reshape(rhs.shape)


def solution(mesh):
    placed = (
        P(None, None, None, "ta", "sa", None),
        P(None, None, None, None, "ta", "sa", None),
        P(None, None, None, "ta", "sa", None),
        P("ta", "sa", None),
    )
    return jax.shard_map(
        functools.partial(shards, mesh.shape["ta"], mesh.shape["sa"]),
        mesh=mesh,
        in_specs=placed,
        out_specs=(P(None, None, None, "ta", "sa", None), P(None, None, None, "ta", "sa", None)),
        check_vma=False,
    )
```

profile of v0, /device:TPU:0, one launch (start us, length us, event | category | flops | bytes accessed | tf_op | source)
XLA Modules:
  0.0 56.0 jit_solution(17155460007957487350)
XLA Ops:
  0.6 0.0 copy-start
  0.6 1.9 %copy-done = bf16[4,2,40,40,1,1,128]{6,3,5,4,2,1,0:T(8,128)(2,1)S(1)} copy-done((bf16[4,2,40,40,1,1,128]{6,3,5,4,2,1,0:T(8,128)(2,1)S(1)}, bf16[4,2,40,40,1,1,128]{6,3,5,4,2,1,0:T(8,128)(2,1)}, u32[]{:S(2)}) %copy-start) | copy-done | bytes 3276824
  2.6 0.0 copy-start.1
  2.6 1.1 %copy-done.1 = bf16[2,40,40,1,1,128]{5,2,4,3,1,0:T(8,128)(2,1)S(1)} copy-done((bf16[2,40,40,1,1,128]{5,2,4,3,1,0:T(8,128)(2,1)S(1)}, bf16[2,40,40,1,1,128]{5,2,4,3,1,0:T(8,128)(2,1)}, u32[]{:S(2)}) %copy-start.1) | copy-done | bytes 819224
  3.7 0.0 copy-start.2
  3.7 0.8 %copy-done.2 = f32[1,2,40,1,1,128]{5,4,3,2,1,0:T(1,128)S(1)} copy-done((f32[1,2,40,1,1,128]{5,4,3,2,1,0:T(1,128)S(1)}, f32[1,2,40,1,1,128]{5,4,3,2,1,0:T(1,128)}, u32[]{:S(2)}) %copy-start.2) | copy-done | bytes 40984
  4.5 0.0 copy-start.3
  4.5 0.7 %copy-done.3 = s32[1,1,2]{2,1,0:T(1,128)S(1)} copy-done((s32[1,1,2]{2,1,0:T(1,128)S(1)}, s32[1,1,2]{2,1,0:T(1,128)}, u32[]{:S(2)}) %copy-start.3) | copy-done | bytes 32
  5.1 49.6 %shard_map.59 = (f32[2,40,128]{2,1,0:T(8,128)S(1)}, f32[2,40,128]{2,1,0:T(8,128)S(1)}) custom-call(f32[2,40,128]{2,1,0:T(8,128)S(1)} %bitcast.12, bf16[4,2,40,40,128]{4,3,2,1,0:T(8,128)(2,1)S(1)} %bitcast.10, bf16[2,40,40,128]{3,2,1,0:T(8,128)(2,1)S(1)} %bitcast.11, s32[2]{0:T(128)S(1)} %bitcast.15), custom_call_target="tpu_custom_call" | custom-call | tf_op jit(solution)/shard_map/pallas_call | solution.py:294
  54.8 0.6 %copy.10 = f32[1,2,40,1,1,128]{5,4,3,2,1,0:T(1,128)} copy(f32[1,2,40,1,1,128]{5,4,3,2,1,0:T(1,128)S(1)} %bitcast.14) | data formatting | bytes 81920
  55.4 0.6 %copy.11 = f32[1,2,40,1,1,128]{5,4,3,2,1,0:T(1,128)} copy(f32[1,2,40,1,1,128]{5,4,3,2,1,0:T(1,128)S(1)} %bitcast.13) | data formatting | bytes 81920
Async XLA Ops:
  0.6 1.9 %copy-start = (bf16[4,2,40,40,1,1,128]{6,3,5,4,2,1,0:T(8,128)(2,1)S(1)}, bf16[4,2,40,40,1,1,128]{6,3,5,4,2,1,0:T(8,128)(2,1)}, u32[]{:S(2)}) copy-start(bf16[4,2,40,40,1,1,128]{6,3,5,4,2,1,0:T(8,128)(2,1)} %param.5) | copy-start | bytes 9830404
  2.6 1.1 %copy-start.1 = (bf16[2,40,40,1,1,128]{5,2,4,3,1,0:T(8,128)(2,1)S(1)}, bf16[2,40,40,1,1,128]{5,2,4,3,1,0:T(8,128)(2,1)}, u32[]{:S(2)}) copy-start(bf16[2,40,40,1,1,128]{5,2,4,3,1,0:T(8,128)(2,1)} %param.6) | copy-start | bytes 2457604
  3.7 0.8 %copy-start.2 = (f32[1,2,40,1,1,128]{5,4,3,2,1,0:T(1,128)S(1)}, f32[1,2,40,1,1,128]{5,4,3,2,1,0:T(1,128)}, u32[]{:S(2)}) copy-start(f32[1,2,40,1,1,128]{5,4,3,2,1,0:T(1,128)} %param.4) | copy-start | bytes 122884
  4.5 0.7 %copy-start.3 = (s32[1,1,2]{2,1,0:T(1,128)S(1)}, s32[1,1,2]{2,1,0:T(1,128)}, u32[]{:S(2)}) copy-start(s32[1,1,2]{2,1,0:T(1,128)} %param.7) | copy-start | bytes 28
where the time goes:
time: 56.3 us; the launch traced here: 56 us
  Pallas kernels  49.6 us (88%)
  local copies, waits for them, and re-layouts  5.73 us (10%)
  between operations  0.65 us (1%)
    pallas_call x1, Pallas kernels, shards(): pl.pallas_call(functools.partial(kernel, nt, nz), out_shape=[jax.ShapeDty...  49.6 us
    unnamed x10, local copies, waits for them, and re-layouts  5.73 us

commit v1 on v0

--- a/solution.py
+++ b/solution.py
@@ -14,18 +14,21 @@
 SWEEPS = 2
 PHASES = 2 * SWEEPS
 UNROLL = 4
+PREPARE_UNROLL = 8
 MESH = pl.DeviceIdType.MESH
 
 
 def kernel(
     nt,
     nz,
-    rhs_ref,
+    rhs_hbm,
     links_ref,
     clover_ref,
-    steps_ref,
+    steps_hbm,
     x_ref,
     r_ref,
+    rhs_ref,
+    steps_ref,
     lk,
     cl,
     g,
@@ -34,6 +37,7 @@
     s_ref,
     e_ref,
     acc,
+    a_ref,
     gv,
     f_ref,
     sbuf,
@@ -52,8 +56,12 @@
 
     copies = [
         pltpu.make_async_copy(links_ref.at[d], lk.at[d], csem.at[d]) for d in range(4)
-    ] + [pltpu.make_async_copy(clover_ref, cl, csem.at[4])]
-    for d in (2, 1, 3, 4, 0):
+    ] + [
+        pltpu.make_async_copy(clover_ref, cl, csem.at[4]),
+        pltpu.make_async_copy(rhs_hbm, rhs_ref, csem.at[5]),
+        pltpu.make_async_copy(steps_hbm, steps_ref, csem.at[6]),
+    ]
+    for d in (5, 1, 2, 0, 3, 4, 6):
         copies[d].start()
 
     barrier = pltpu.get_barrier_semaphore()
@@ -78,6 +86,7 @@
     def roll(v, by):
         return pltpu.roll(v, by % lanes, 1)
 
+    copies[5].wait()
     for c in range(2):
         v = rhs_ref[c]
         w = roll(v, half)
@@ -87,28 +96,28 @@
         xs[1, c] = zero
 
     def prepare(plain, rolled, groups):
-        def body(i, carry):
-            for c in range(2):
-                b = roll(rolled(c, i).astype(jnp.float32), half)
-                for source, group in zip(plain, groups):
-                    a = source(c, i).astype(jnp.float32)
-                    g[group, 0, c, i] = jnp.where(low, a, b)
-                    g[group, 1, c, i] = jnp.where(low, b, a)
+        def body(outer, carry):
+            for inner in range(PREPARE_UNROLL):
+                i = outer * PREPARE_UNROLL + inner
+                for c in range(2):
+                    b = roll(rolled(c, i).astype(jnp.float32), half)
+                    for source, group in zip(plain, groups):
+                        a = source(c, i).astype(jnp.float32)
+                        g[group, 0, c, i] = jnp.where(low, a, b)
+                        g[group, 1, c, i] = jnp.where(low, b, a)
             return carry
 
-        lax.fori_loop(0, dof, body, 0)
+        lax.fori_loop(0, dof // PREPARE_UNROLL, body, 0)
 
     def link(d):
         return lambda c, i: lk[d, c, i]
 
-    copies[2].wait()
-    copies[1].wait()
-    prepare([link(2)], link(1), [0])
-    copies[3].wait()
-    copies[4].wait()
-    copies[0].wait()
+    for d in (1, 2, 0):
+        copies[d].wait()
+    prepare([link(2), link(0)], link(1), [0, 3])
+    for d in (3, 4, 6):
+        copies[d].wait()
     prepare([lambda c, i: cl[c, i], link(0)], link(3), [1, 2])
-    prepare([link(0)], link(1), [3])
 
     def fold(v):
         total = v[0:8]
@@ -116,18 +125,17 @@
             total = total + v[8 * t : 8 * t + 8]
         return total
 
-    def gathered(slots):
+    def gathered(slot):
         parts = []
         for t in range(tiles):
             total = None
-            for slot in slots:
-                for k in range(8):
-                    piece = f_ref[slot, pl.ds(8 * 8 * t + k, 8, stride=8), :]
-                    total = piece if total is None else total + piece
+            for k in range(8):
+                piece = f_ref[slot, pl.ds(8 * 8 * t + k, 8, stride=8), :]
+                total = piece if total is None else total + piece
             parts.append(total)
         return jnp.concatenate(parts, axis=0)
 
-    def sweep_matrices(forward, forward_half, inputs, backward, backward_half, slot):
+    def sweep_matrices(forward, forward_half, inputs, backward, backward_half, more):
         vr, vi = inputs
         vs = vr + vi
         shared = backward == forward
@@ -139,8 +147,12 @@
             p2 = fold(mi * vi)
             p3 = fold(ms * vs)
             at = pl.multiple_of(8 * i, 8)
-            f_ref[slot, pl.ds(at, 8), :] = p1 - p2
-            f_ref[slot + 1, pl.ds(at, 8), :] = p3 - p1 - p2
+            real_part, imag_part = p1 - p2, p3 - p1 - p2
+            if more:
+                real_part = real_part + f_ref[0, pl.ds(at, 8), :]
+                imag_part = imag_part + f_ref[1, pl.ds(at, 8), :]
+            f_ref[0, pl.ds(at, 8), :] = real_part
+            f_ref[1, pl.ds(at, 8), :] = imag_part
             if backward is None:
                 return carry
             if not shared:
@@ -171,11 +183,20 @@
         first = (lane // half) == h
         h_is_0 = (lane * 0 + h) == 0
 
+        def ahead(v):
+            n = -v
+            ya = jnp.where(y_last, roll(n, (LY - 1) * LX), roll(n, -LX))
+            za = jnp.where(z_last, 0.0, roll(n, -plane))
+            xa = jnp.where(x_last, roll(n, LX - 1), roll(n, -1))
+            return jnp.where(first, ya, za), jnp.where(first, v, xa)
+
         for c in range(2):
-            s_ref[c] = rs[h, c]
+            v = rs[h, c]
+            s_ref[c] = v
             e_ref[c] = zero
             acc[0, c] = zero
             acc[1, c] = zero
+            a_ref[0, c], a_ref[1, c] = ahead(v)
 
         def step(k, carry):
             sr, si = s_ref[0], s_ref[1]
@@ -183,29 +204,18 @@
             gv[0] = gr
             gv[1] = gi
             gv[2] = gr - gi
-
-            def ahead0(v):
-                n = -v
-                ya = jnp.where(y_last, roll(n, (LY - 1) * LX), roll(n, -LX))
-                za = jnp.where(z_last, 0.0, roll(n, -plane))
-                return jnp.where(first, ya, za)
-
-            def ahead1(v):
-                n = -v
-                xa = jnp.where(x_last, roll(n, LX - 1), roll(n, -1))
-                return jnp.where(first, v, xa)
-
-            back0 = sweep_matrices(0, h, (ahead0(sr), ahead0(si)), 0, h, 0)
-            back2 = sweep_matrices(1, h, (ahead1(sr), ahead1(si)), 2, h, 2)
+            back0 = sweep_matrices(0, h, (a_ref[0, 0], a_ref[0, 1]), 0, h, False)
+            back2 = sweep_matrices(1, h, (a_ref[1, 0], a_ref[1, 1]), 2, h, True)
             q = []
             for c in range(2):
                 b, d = back0[c], back2[c]
                 yb = jnp.where(y_first, roll(b, -(LY - 1) * LX), roll(b, LX))
                 zb = jnp.where(z_first, 0.0, roll(b, plane))
                 xb = jnp.where(x_first, roll(d, -(LX - 1)), roll(d, 1))
-                u = gathered((c, 2 + c)) + jnp.where(first, yb, zb) + jnp.where(first, 0.0, xb)
+                u = gathered(c) + jnp.where(first, yb, zb) + jnp.where(first, 0.0, xb)
                 q.append(u + roll(u, half))
             qr, qi = q
+            ahead_r, ahead_i = ahead(qr), ahead(qi)
 
             def total(v):
                 return jnp.sum(jnp.sum(fold(v), axis=0, keepdims=True), axis=1, keepdims=True)
@@ -220,6 +230,9 @@
             e_ref[1] += ar * si + ai * sr
             s_ref[0] = sr - (ar * qr - ai * qi)
             s_ref[1] = si - (ar * qi + ai * qr)
+            for n in range(2):
+                a_ref[n, 0] -= ar * ahead_r[n] - ai * ahead_i[n]
+                a_ref[n, 1] -= ar * ahead_i[n] + ai * ahead_r[n]
             for n, (vr, vi) in enumerate((back0, back2)):
                 acc[n, 0] += ar * vr - ai * vi
                 acc[n, 1] += ar * vi + ai * vr
@@ -257,26 +270,41 @@
             xs[h, c] += ec
             rs[h, c] = s_ref[c]
 
-        for send in sends:
-            send.wait()
-
         def unpack(n):
             m = rbuf[ph, n]
             w = roll(m, half)
             return jnp.where(low, m, w), jnp.where(low, w, m)
 
-        got_t, got_e, got_b = unpack(0), unpack(1), unpack(2)
-        inputs = []
-        for c, ec in enumerate((er, ei)):
-            tin = jnp.where(h_is_0, got_t[c], ec)
-            zin = jnp.where(z_last, roll(got_e[c], -plane), 0.0)
-            inputs.append(jnp.where(first, zin, tin))
-        sweep_matrices(3, other, inputs, None, None, 0)
-        for c in range(2):
-            u = gathered((c,))
-            behind = jnp.where(h_is_0, bt[c], got_t[c])
-            zb = jnp.where(z_first, roll(got_b[c], plane), 0.0)
-            rs[other, c] += u + roll(u, half) + behind + zb
+        sends[1].wait()
+        sends[2].wait()
+        got_e, got_b = unpack(1), unpack(2)
+
+        def hop(times):
+            inputs = []
+            for c in range(2):
+                zin = jnp.where(z_last, roll(got_e[c], -plane), 0.0)
+                inputs.append(jnp.where(first, zin, times[c]))
+            sweep_matrices(3, other, inputs, None, None, False)
+            for c in range(2):
+                u = gathered(c)
+                zb = jnp.where(z_first, roll(got_b[c], plane), 0.0)
+                rs[other, c] += u + roll(u, half) + zb
+
+        @pl.when(h == 0)
+        def _():
+            for c in range(2):
+                rs[1, c] += bt[c]
+            sends[0].wait()
+            hop(unpack(0))
+
+        @pl.when(h == 1)
+        def _():
+            hop((er, ei))
+            sends[0].wait()
+            got_t = unpack(0)
+            for c in range(2):
+                rs[0, c] += got_t[c]
+
         return token
 
     lax.fori_loop(0, PHASES, phase, 0)
@@ -290,13 +318,15 @@
     dof, lanes = rhs.shape[2], rhs.shape[-1]
     f32 = jnp.float32
     vmem = pl.BlockSpec(memory_space=pltpu.VMEM)
-    hbm = pl.BlockSpec(memory_space=pl.ANY)
+    hbm = pl.BlockSpec(memory_space=pltpu.HBM)
     x, r = pl.pallas_call(
         functools.partial(kernel, nt, nz),
         out_shape=[jax.ShapeDtypeStruct((2, dof, lanes), f32)] * 2,
-        in_specs=[vmem, hbm, hbm, pl.BlockSpec(memory_space=pltpu.SMEM)],
+        in_specs=[hbm, hbm, hbm, hbm],
         out_specs=[vmem, vmem],
         scratch_shapes=[
+            pltpu.VMEM((2, dof, lanes), f32),
+            pltpu.SMEM((2,), jnp.int32),
             pltpu.VMEM((4, 2, dof, dof, lanes), jnp.bfloat16),
             pltpu.VMEM((2, dof, dof, lanes), jnp.bfloat16),
             pltpu.VMEM((4, 2, 2, dof, dof, lanes), f32),
@@ -305,16 +335,17 @@
             pltpu.VMEM((2, dof, lanes), f32),
             pltpu.VMEM((2, dof, lanes), f32),
             pltpu.VMEM((2, 2, dof, lanes), f32),
+            pltpu.VMEM((2, 2, dof, lanes), f32),
             pltpu.VMEM((3, dof, lanes), f32),
-            pltpu.VMEM((4, 8 * dof, lanes), f32),
+            pltpu.VMEM((2, 8 * dof, lanes), f32),
             pltpu.VMEM((PHASES, 3, dof, lanes), f32),
             pltpu.VMEM((PHASES, 3, dof, lanes), f32),
-            pltpu.SemaphoreType.DMA((5,)),
+            pltpu.SemaphoreType.DMA((7,)),
             pltpu.SemaphoreType.DMA((PHASES, 3)),
             pltpu.SemaphoreType.DMA((PHASES, 3)),
         ],
         compiler_params=pltpu.CompilerParams(
-            collective_id=0, has_side_effects=True, vmem_limit_bytes=48 * 1024 * 1024
+            collective_id=0, has_side_effects=True, vmem_limit_bytes=67043328
         ),
     )(
         rhs.reshape(2, dof, lanes),

time: 56.3 us -> 45.9 us (0.82)
  Pallas kernels: 49.6 us -> 42.2 us
  local copies, waits for them, and re-layouts: 5.73 us -> 2.8 us
    pallas_call x1, Pallas kernels: 49.6 us -> 42.2 us  [shards(): pl.pallas_call(functools.partial(kernel, nt, nz), out_shape=[jax.ShapeDty...]
    unnamed x10 -> x2, local copies, waits for them, and re-layouts: 5.73 us -> 2.8 us
where the time goes in v1:
time: 45.9 us; the launch traced here: 45.6 us
  Pallas kernels  42.2 us (92%)
  local copies, waits for them, and re-layouts  2.8 us (6%)
  between operations  0.64 us (1%)
    pallas_call x1, Pallas kernels, shards(): pl.pallas_call(functools.partial(kernel, nt, nz), out_shape=[jax.ShapeDty...  42.2 us
    unnamed x2, local copies, waits for them, and re-layouts  2.8 us

profile of v1, /device:TPU:0, one launch (start us, length us, event | category | flops | bytes accessed | tf_op | source)
XLA Modules:
  0.0 45.6 jit_solution(7642469105868486798)
XLA Ops:
  0.6 42.2 %shard_map.59 = (f32[2,40,128]{2,1,0:T(8,128)}, f32[2,40,128]{2,1,0:T(8,128)}) custom-call(f32[2,40,128]{2,1,0:T(8,128)} %bitcast.12, bf16[4,2,40,40,128]{4,3,2,1,0:T(8,128)(2,1)} %bitcast.10, bf16[2,40,40,128]{3,2,1,0:T(8,128)(2,1)} %bitcast.11, s32[2]{0:T(128)} %bitcast.15), custom_call_target="tpu_custom_call" | custom-call | tf_op jit(solution)/shard_map/pallas_call | solution.py:322
  42.8 1.4 %copy.10 = f32[1,2,40,1,1,128]{5,4,3,2,1,0:T(1,128)} copy(f32[1,2,40,1,1,128]{5,4,3,2,1,0:T(1,128)} %bitcast.14) | data formatting | bytes 81920
  44.2 1.4 %copy.11 = f32[1,2,40,1,1,128]{5,4,3,2,1,0:T(1,128)} copy(f32[1,2,40,1,1,128]{5,4,3,2,1,0:T(1,128)} %bitcast.13) | data formatting | bytes 81920

commit v2 on v1

--- a/solution.py
+++ b/solution.py
@@ -13,7 +13,7 @@
 MR_MAX = 3
 SWEEPS = 2
 PHASES = 2 * SWEEPS
-UNROLL = 4
+UNROLL = 10
 PREPARE_UNROLL = 8
 MESH = pl.DeviceIdType.MESH
 
@@ -198,7 +198,7 @@
             acc[1, c] = zero
             a_ref[0, c], a_ref[1, c] = ahead(v)
 
-        def step(k, carry):
+        def images():
             sr, si = s_ref[0], s_ref[1]
             gr, gi = signs * sr, signs * si
             gv[0] = gr
@@ -216,59 +216,89 @@
                 q.append(u + roll(u, half))
             qr, qi = q
             ahead_r, ahead_i = ahead(qr), ahead(qi)
-
-            def total(v):
-                return jnp.sum(jnp.sum(fold(v), axis=0, keepdims=True), axis=1, keepdims=True)
-
+            return sr, si, qr, qi, ahead_r, ahead_i, back0, back2
+
+        def total(v):
+            return jnp.sum(jnp.sum(fold(v), axis=0, keepdims=True), axis=1, keepdims=True)
+
+        def scale(k, sr, si, qr, qi):
             numer_real = total(qr * sr + qi * si)
             numer_imag = total(qr * si - qi * sr)
             denom = total(qr * qr + qi * qi) + 2e-6
             live = (lane * 0 + limit) > k
             ar = jnp.where(live, jnp.broadcast_to(numer_real / denom, shape), 0.0)
             ai = jnp.where(live, jnp.broadcast_to(numer_imag / denom, shape), 0.0)
-            e_ref[0] += ar * sr - ai * si
-            e_ref[1] += ar * si + ai * sr
-            s_ref[0] = sr - (ar * qr - ai * qi)
-            s_ref[1] = si - (ar * qi + ai * qr)
-            for n in range(2):
-                a_ref[n, 0] -= ar * ahead_r[n] - ai * ahead_i[n]
-                a_ref[n, 1] -= ar * ahead_i[n] + ai * ahead_r[n]
-            for n, (vr, vi) in enumerate((back0, back2)):
-                acc[n, 0] += ar * vr - ai * vi
-                acc[n, 1] += ar * vi + ai * vr
+            return ar, ai
+
+        def times(ar, ai, v):
+            return ar * v[0] - ai * v[1], ar * v[1] + ai * v[0]
+
+        def step(k, carry):
+            sr, si, qr, qi, ahead_r, ahead_i, back0, back2 = images()
+            ar, ai = scale(k, sr, si, qr, qi)
+            es = times(ar, ai, (sr, si))
+            qs = times(ar, ai, (qr, qi))
+            for c, old in enumerate((sr, si)):
+                e_ref[c] += es[c]
+                s_ref[c] = old - qs[c]
+            for n, back in enumerate((back0, back2)):
+                moved = times(ar, ai, (ahead_r[n], ahead_i[n]))
+                added = times(ar, ai, back)
+                for c in range(2):
+                    a_ref[n, c] -= moved[c]
+                    acc[n, c] += added[c]
             return carry
 
-        lax.fori_loop(0, MR_MAX, step, 0)
-
-        er, ei = e_ref[0], e_ref[1]
-        bz = [-jnp.where(first, roll(acc[0, c], half), acc[0, c]) for c in range(2)]
-        bt = [-jnp.where(first, acc[1, c], roll(acc[1, c], half)) for c in range(2)]
-        packed = jnp.where(low, er, ei)
-        sbuf[ph, 0] = jnp.where(h_is_0, packed, jnp.where(low, bt[0], bt[1]))
-        sbuf[ph, 1] = packed
-        sbuf[ph, 2] = jnp.where(low, bz[0], bz[1])
-
-        @pl.when(ph == 0)
-        def _():
-            pl.semaphore_wait(barrier, 4)
-
-        target = lax.rem(ta + nt + 2 * h - 1, nt)
-        sends = []
-        for n, where_to in enumerate(({"ta": target}, {"sa": z_prev}, {"sa": z_next})):
-            send = pltpu.make_async_remote_copy(
-                src_ref=sbuf.at[ph, n],
-                dst_ref=rbuf.at[ph, n],
+        lax.fori_loop(0, MR_MAX - 1, step, 0)
+
+        def pack(v):
+            return jnp.where(low, v[0], v[1])
+
+        def bt_of(v):
+            return [-jnp.where(first, v[c], roll(v[c], half)) for c in range(2)]
+
+        def sender(n, where_to, src, dst):
+            return pltpu.make_async_remote_copy(
+                src_ref=src,
+                dst_ref=dst,
                 send_sem=ssem.at[ph, n],
                 recv_sem=rsem.at[ph, n],
                 device_id=where_to,
                 device_id_type=MESH,
             )
-            send.start()
-            sends.append(send)
-
-        for c, ec in enumerate((er, ei)):
-            xs[h, c] += ec
-            rs[h, c] = s_ref[c]
+
+        target = {"ta": lax.rem(ta + nt + 2 * h - 1, nt)}
+        e_old = (e_ref[0], e_ref[1])
+
+        @pl.when(ph == 0)
+        def _():
+            pl.semaphore_wait(barrier, 4)
+
+        sr, si, qr, qi, _, _, back0, back2 = images()
+        ar, ai = scale(MR_MAX - 1, sr, si, qr, qi)
+        es = times(ar, ai, (sr, si))
+        e_new = [e_old[c] + es[c] for c in range(2)]
+        added = times(ar, ai, back2)
+        bt = bt_of([acc[1, c] + added[c] for c in range(2)])
+        sbuf[ph, 0] = jnp.where(h_is_0, pack(e_new), pack(bt))
+        sends = [sender(0, target, sbuf.at[ph, 0], rbuf.at[ph, 0])]
+        sends[0].start()
+        bs = times(ar, ai, back0)
+        bz = []
+        for c in range(2):
+            v = acc[0, c] + bs[c]
+            bz.append(-jnp.where(first, roll(v, half), v))
+        sbuf[ph, 1] = pack(e_new)
+        sbuf[ph, 2] = pack(bz)
+        sends.append(sender(1, {"sa": z_prev}, sbuf.at[ph, 1], rbuf.at[ph, 1]))
+        sends.append(sender(2, {"sa": z_next}, sbuf.at[ph, 2], rbuf.at[ph, 2]))
+        sends[1].start()
+        sends[2].start()
+
+        qs = times(ar, ai, (qr, qi))
+        for c, old in enumerate((sr, si)):
+            xs[h, c] += e_new[c]
+            rs[h, c] = old - qs[c]
 
         def unpack(n):
             m = rbuf[ph, n]
@@ -299,7 +329,7 @@
 
         @pl.when(h == 1)
         def _():
-            hop((er, ei))
+            hop(e_new)
             sends[0].wait()
             got_t = unpack(0)
             for c in range(2):

time: 45.9 us -> 43.7 us (0.952)
  Pallas kernels: 42.2 us -> 40.1 us
    pallas_call x1, Pallas kernels: 42.2 us -> 40.1 us  [shards(): pl.pallas_call(functools.partial(kernel, nt, nz), out_shape=[jax.ShapeDty...]
where the time goes in v2:
time: 43.7 us; the launch traced here: 43.5 us
  Pallas kernels  40.1 us (92%)
  local copies, waits for them, and re-layouts  2.8 us (6%)
  between operations  0.64 us (1%)
    pallas_call x1, Pallas kernels, shards(): pl.pallas_call(functools.partial(kernel, nt, nz), out_shape=[jax.ShapeDty...  40.1 us
    unnamed x2, local copies, waits for them, and re-layouts  2.8 us

profile of v2, /device:TPU:0, one launch (start us, length us, event | category | flops | bytes accessed | tf_op | source)
XLA Modules:
  0.0 43.5 jit_solution(8879362740740342734)
XLA Ops:
  0.6 40.1 %shard_map.59 = (f32[2,40,128]{2,1,0:T(8,128)}, f32[2,40,128]{2,1,0:T(8,128)}) custom-call(f32[2,40,128]{2,1,0:T(8,128)} %bitcast.12, bf16[4,2,40,40,128]{4,3,2,1,0:T(8,128)(2,1)} %bitcast.10, bf16[2,40,40,128]{3,2,1,0:T(8,128)(2,1)} %bitcast.11, s32[2]{0:T(128)} %bitcast.15), custom_call_target="tpu_custom_call" | custom-call | tf_op jit(solution)/shard_map/pallas_call | solution.py:352
  40.7 1.4 %copy.10 = f32[1,2,40,1,1,128]{5,4,3,2,1,0:T(1,128)} copy(f32[1,2,40,1,1,128]{5,4,3,2,1,0:T(1,128)} %bitcast.14) | data formatting | bytes 81920
  42.1 1.4 %copy.11 = f32[1,2,40,1,1,128]{5,4,3,2,1,0:T(1,128)} copy(f32[1,2,40,1,1,128]{5,4,3,2,1,0:T(1,128)} %bitcast.13) | data formatting | bytes 81920
